TPU v7x, 256 devices: a whole 4x4x8 slice. The times are simulated.
256 devices in a mesh: row: 32 (over z_hi, x, core), col: 8 (over y, z_lo).
Axes of the slice: x: 4, y: 4, z: 8 (z_hi: 4, z_lo: 2; z = z_hi * 2 + z_lo), core: 2. Of those that a mesh axis runs over, the one named last changes fastest.
Arguments:
- pivots: int32 [256], replicated, may hold values from 0 to 32767, as said below
- panel: float32 [32768, 256], P(('row', 'col')), may hold values from -6 to 6
- prior: bfloat16 [32768, 3072], P(('row', 'col')), may hold values from -0.796875 to 0.796875
- finished: bfloat16 [32768, 256], P(('row', 'col')), may hold values from -6 to 6
- pairs: int32 [32768], replicated, may hold values from 0 to 639999, as said below
- occupied: bfloat16 [800, 120], replicated, may hold values from -0.21875 to 0.21875
Outputs:
- updated: float32 [32768, 256], P(('row', 'col'))
- halves: float32 [256, 120, 800], P(('row', 'col'))
Inputs may be any that keep to these rules, and one draw needn't show every extreme that they name: `pivots`: distinct rows; at most 2 of them lie among the rows of one device (aligned blocks of 128 rows), and one device holds exactly 2. `pairs`: each value a * 800 + b with 0 <= b <= a < 800; all distinct and increasing.
All inputs are finite; a program needn't handle non-finite values.
Results may differ from a plain program's by a relative error of at most 0.0003.
Values may be sent and summed in bfloat16 or wider, within the bound.
A program may use at most 64 MiB of HBM per device.

v0:
```python
import jax
import jax.numpy as jnp
from jax import lax
from jax.sharding import PartitionSpec as P


def half_transform(received, pair_ids, occupied):
    orbitals = occupied.shape[0]
    pair_count = received.shape[0]
    vector_count = received.shape[1]
    first_ao = pair_ids // orbitals
    second_ao = pair_ids % orbitals
    off_diag = first_ao != second_ao
    occ_first = jnp.take(occupied, first_ao, axis=0)
    occ_second = jnp.where(
        off_diag[:, None], jnp.take(occupied, second_ao, axis=0), jnp.zeros((), jnp.bfloat16)
    )
    coeffs = jnp.concatenate([occ_first, occ_second], axis=0)
    targets = jnp.concatenate([second_ao, first_ao], axis=0).astype(jnp.int32)
    entries = jnp.concatenate([received, received], axis=0)
    doubled = 2 * pair_count
    wanted = min(doubled, max(1024, doubled // 8))
    block_rows = wanted
    for candidate in range(wanted, 0, -1):
        if doubled % candidate == 0:
            block_rows = candidate
            break
    columns = jnp.arange(orbitals, dtype=jnp.int32)

    def one_block(block_index, accumulated):
        start = block_index * block_rows
        coeff_block = lax.dynamic_slice_in_dim(coeffs, start, block_rows, 0)
        target_block = lax.dynamic_slice_in_dim(targets, start, block_rows, 0)
        entry_block = lax.dynamic_slice_in_dim(entries, start, block_rows, 0)
        matches = target_block[:, None] == columns[None, :]
        spread = jnp.where(
            matches[None, :, :], entry_block.T[:, :, None], jnp.zeros((), jnp.bfloat16)
        )
        return accumulated + jnp.einsum(
            "pi,vpm->vim", coeff_block, spread, preferred_element_type=jnp.float32
        )

    initial = jnp.zeros((vector_count, occupied.shape[1], orbitals), jnp.float32)
    return lax.fori_loop(0, doubled // block_rows, one_block, initial)


def per_device(pivots, panel, prior, finished, pairs, occupied):
    rows_dev = prior.shape[0]
    row_count = lax.axis_size("row")
    col_count = lax.axis_size("col")
    own_index = lax.axis_index("row") * col_count + lax.axis_index("col")
    owner = pivots // rows_dev
    local_rows = pivots % rows_dev
    owned = owner == own_index
    picked = jnp.take(prior, local_rows, axis=0).astype(jnp.float32)
    contribution = jnp.where(owned[:, None], picked, jnp.zeros_like(picked))
    pivot_rows = lax.psum(contribution, ("row", "col")).astype(jnp.bfloat16)
    updated = panel - lax.dot_general(
        prior, pivot_rows, (((1,), (1,)), ((), ())), preferred_element_type=jnp.float32
    )
    by_device = pairs.reshape(row_count, col_count, rows_dev)
    col_pairs = lax.dynamic_slice_in_dim(by_device, lax.axis_index("col"), 1, 1).reshape(-1)
    grouped = finished.reshape(rows_dev, row_count, finished.shape[1] // row_count)
    received = lax.all_to_all(grouped, "row", split_axis=1, concat_axis=0, tiled=True)
    partials = half_transform(
        received.reshape(received.shape[0], received.shape[2]), col_pairs, occupied
    )
    halves = lax.psum_scatter(partials, "col", scatter_dimension=0, tiled=True)
    return (updated, halves)


def solution(mesh):
    return jax.shard_map(
        per_device,
        mesh=mesh,
        in_specs=(
            P(),
            P(("row", "col"), None),
            P(("row", "col"), None),
            P(("row", "col"), None),
            P(),
            P(),
        ),
        out_specs=(P(("row", "col"), None), P(("row", "col"), None, None)),
        check_vma=False,
    )
```

profile of v0, /device:TPU:32, one launch (start us, length us, event | category | flops | bytes accessed | tf_op | source)
XLA Modules:
  0.0 254.6 jit_solution(17810283203826027613)
XLA Ops:
  7.2 0.0 copy-start
  7.2 0.0 copy-start.1
  7.2 1.7 copy.17
  8.9 10.4 %all-to-all-start = ((bf16[128,32,8]{0,2,1:T(8,128)(2,1)}), bf16[128,32,8]{0,2,1:T(8,128)(2,1)S(1)}, u32[]{:S(2)}, u32[]{:S(2)}) async-start(bf16[128,32,8]{0,2,1:T(8,128)(2,1)} %bitcast.4), calls=%async_computation | async-start | bytes 131072 | tf_op jit(solution)/shard_map/all_to_all | solution.py:64
  19.3 0.0 reduce-scatter.2.cloned.1.call-start
  19.3 1.0 broadcast_remainder_fusion
  20.3 1.0 compare_reduce_fusion
  21.4 0.0 copy-done.1
  21.4 12.1 %gather_fusion.2 = bf16[4096,120]{1,0:T(8,128)(2,1)S(1)} fusion(bf16[800,120]{1,0:T(8,128)(2,1)S(1)} %copy-done.1, s32[4096]{0:T(1024)S(1)} %get-tuple-element.172), kind=kCustom, calls=%fused_computation.1.clone | custom fusion | bytes 1982464 | tf_op jit(solution)/shard_map/jit(_take)/gather | solution.py:16
  33.5 12.1 %gather_fusion.1 = bf16[4096,120]{1,0:T(8,128)(2,1)S(1)} fusion(bf16[800,120]{1,0:T(8,128)(2,1)S(1)} %copy-done.1, s32[4096]{0:T(1024)S(1)} %fusion.21), kind=kCustom, calls=%fused_computation.clone | custom fusion | bytes 1982464 | tf_op jit(solution)/shard_map/jit(_take)/gather | solution.py:14
  45.7 2.1 broadcast_select_fusion
  47.8 1.4 select_select_fusion
  49.2 0.4 pad_maximum_fusion
  49.7 3.0 %copy.18 = bf16[8192,120]{0,1:T(8,128)(2,1)} copy(bf16[8192,120]{1,0:T(8,128)(2,1)S(1)} %pad_maximum_fusion) | data formatting | bytes 3932160
  52.6 0.0 all-to-all-done
  52.7 55.6 %while.14 = (s32[]{:T(128)}, f32[8,120,800]{1,2,0:T(8,128)}, s32[8192]{0:T(1024)S(1)}, bf16[8192,8]{0,1:T(8,128)(2,1)S(1)}, bf16[8192,120]{0,1:T(8,128)(2,1)}, /*index=5*/s32[]{:T(128)}, s32[]{:T(128)}, s32[]{:T(128)}, s32[]{:T(128)}) while((s32[]{:T(128)}, f32[8,120,800]{1,2,0:T(8,128)}, s32[8192]{0:T(1024)S(1)}, ...), condition=%wide.region_2.4_spmd.clone, body=%wide.region_1.3_spmd.clone.sunk | while | flops 1581772800 | bytes 8294561 | solution.py:44
  52.7 0.6 iota_compare_fusion.2
  53.3 5.9 %bitcast_add_fusion.2 = f32[8,120,800]{1,2,0:T(8,128)} fusion(f32[8,120,800]{1,2,0:T(8,128)} %get-tuple-element.216, pred[1024,800]{0,1:T(8,128)(4,1)S(1)} %iota_compare_fusion.2, bf16[8,1024]{1,0:T(8,128)(2,1)S(1)} %dynamic-slice_bitcast_fusion.2, pred[]{:T(512)S(6)} %compare.6, bf16[8192,120]{0,1:T(8,128)(2,1)} %get-tuple-element.228, ...), kind=kOutput, calls=%fused_computation.9.clone.1 | convolution fusion | flops 1580953600 | bytes 7430149 | tf_op jit(solution)/shard_map/while/body/eval_jaxpr/pi,vpm->vim/dot_general | solution.py:39
  59.2 0.6 iota_compare_fusion.2
  59.9 6.4 %bitcast_add_fusion.2 = f32[8,120,800]{1,2,0:T(8,128)} fusion(f32[8,120,800]{1,2,0:T(8,128)} %get-tuple-element.216, pred[1024,800]{0,1:T(8,128)(4,1)S(1)} %iota_compare_fusion.2, bf16[8,1024]{1,0:T(8,128)(2,1)S(1)} %dynamic-slice_bitcast_fusion.2, pred[]{:T(512)S(6)} %compare.6, bf16[8192,120]{0,1:T(8,128)(2,1)} %get-tuple-element.228, ...), kind=kOutput, calls=%fused_computation.9.clone.1 | convolution fusion | flops 1580953600 | bytes 7430149 | tf_op jit(solution)/shard_map/while/body/eval_jaxpr/pi,vpm->vim/dot_general | solution.py:39
  66.2 0.6 iota_compare_fusion.2
  66.9 6.4 %bitcast_add_fusion.2 = f32[8,120,800]{1,2,0:T(8,128)} fusion(f32[8,120,800]{1,2,0:T(8,128)} %get-tuple-element.216, pred[1024,800]{0,1:T(8,128)(4,1)S(1)} %iota_compare_fusion.2, bf16[8,1024]{1,0:T(8,128)(2,1)S(1)} %dynamic-slice_bitcast_fusion.2, pred[]{:T(512)S(6)} %compare.6, bf16[8192,120]{0,1:T(8,128)(2,1)} %get-tuple-element.228, ...), kind=kOutput, calls=%fused_computation.9.clone.1 | convolution fusion | flops 1580953600 | bytes 7430149 | tf_op jit(solution)/shard_map/while/body/eval_jaxpr/pi,vpm->vim/dot_general | solution.py:39
  73.2 0.6 iota_compare_fusion.2
  73.9 6.4 %bitcast_add_fusion.2 = f32[8,120,800]{1,2,0:T(8,128)} fusion(f32[8,120,800]{1,2,0:T(8,128)} %get-tuple-element.216, pred[1024,800]{0,1:T(8,128)(4,1)S(1)} %iota_compare_fusion.2, bf16[8,1024]{1,0:T(8,128)(2,1)S(1)} %dynamic-slice_bitcast_fusion.2, pred[]{:T(512)S(6)} %compare.6, bf16[8192,120]{0,1:T(8,128)(2,1)} %get-tuple-element.228, ...), kind=kOutput, calls=%fused_computation.9.clone.1 | convolution fusion | flops 1580953600 | bytes 7430149 | tf_op jit(solution)/shard_map/while/body/eval_jaxpr/pi,vpm->vim/dot_general | solution.py:39
  80.3 0.6 iota_compare_fusion.2
  80.9 6.4 %bitcast_add_fusion.2 = f32[8,120,800]{1,2,0:T(8,128)} fusion(f32[8,120,800]{1,2,0:T(8,128)} %get-tuple-element.216, pred[1024,800]{0,1:T(8,128)(4,1)S(1)} %iota_compare_fusion.2, bf16[8,1024]{1,0:T(8,128)(2,1)S(1)} %dynamic-slice_bitcast_fusion.2, pred[]{:T(512)S(6)} %compare.6, bf16[8192,120]{0,1:T(8,128)(2,1)} %get-tuple-element.228, ...), kind=kOutput, calls=%fused_computation.9.clone.1 | convolution fusion | flops 1580953600 | bytes 7430149 | tf_op jit(solution)/shard_map/while/body/eval_jaxpr/pi,vpm->vim/dot_general | solution.py:39
  87.3 0.6 iota_compare_fusion.2
  87.9 6.4 %bitcast_add_fusion.2 = f32[8,120,800]{1,2,0:T(8,128)} fusion(f32[8,120,800]{1,2,0:T(8,128)} %get-tuple-element.216, pred[1024,800]{0,1:T(8,128)(4,1)S(1)} %iota_compare_fusion.2, bf16[8,1024]{1,0:T(8,128)(2,1)S(1)} %dynamic-slice_bitcast_fusion.2, pred[]{:T(512)S(6)} %compare.6, bf16[8192,120]{0,1:T(8,128)(2,1)} %get-tuple-element.228, ...), kind=kOutput, calls=%fused_computation.9.clone.1 | convolution fusion | flops 1580953600 | bytes 7430149 | tf_op jit(solution)/shard_map/while/body/eval_jaxpr/pi,vpm->vim/dot_general | solution.py:39
  94.3 0.6 iota_compare_fusion.2
  94.9 6.4 %bitcast_add_fusion.2 = f32[8,120,800]{1,2,0:T(8,128)} fusion(f32[8,120,800]{1,2,0:T(8,128)} %get-tuple-element.216, pred[1024,800]{0,1:T(8,128)(4,1)S(1)} %iota_compare_fusion.2, bf16[8,1024]{1,0:T(8,128)(2,1)S(1)} %dynamic-slice_bitcast_fusion.2, pred[]{:T(512)S(6)} %compare.6, bf16[8192,120]{0,1:T(8,128)(2,1)} %get-tuple-element.228, ...), kind=kOutput, calls=%fused_computation.9.clone.1 | convolution fusion | flops 1580953600 | bytes 7430149 | tf_op jit(solution)/shard_map/while/body/eval_jaxpr/pi,vpm->vim/dot_general | solution.py:39
  101.3 0.6 iota_compare_fusion.2
  101.9 6.4 %bitcast_add_fusion.2 = f32[8,120,800]{1,2,0:T(8,128)} fusion(f32[8,120,800]{1,2,0:T(8,128)} %get-tuple-element.216, pred[1024,800]{0,1:T(8,128)(4,1)S(1)} %iota_compare_fusion.2, bf16[8,1024]{1,0:T(8,128)(2,1)S(1)} %dynamic-slice_bitcast_fusion.2, pred[]{:T(512)S(6)} %compare.6, bf16[8192,120]{0,1:T(8,128)(2,1)} %get-tuple-element.228, ...), kind=kOutput, calls=%fused_computation.9.clone.1 | convolution fusion | flops 1580953600 | bytes 7430149 | tf_op jit(solution)/shard_map/while/body/eval_jaxpr/pi,vpm->vim/dot_general | solution.py:39
  108.3 0.0 copy-start.3
  108.3 0.0 reduce-scatter.2.cloned.1.call-update
  108.3 0.6 copy-done.3
  109.0 0.0 copy-done
  109.0 1.6 gather_fusion
  110.6 0.0 copy-start.2
  110.6 2.4 convert_select_fusion
  113.0 0.0 copy-done.2
  113.0 0.1 copy.16
  113.1 133.3 %all-reduce.1 = bf16[256,3072]{1,0:T(8,128)(2,1)S(1)} all-reduce(f32[256,3072]{1,0:T(8,128)} %convert_select_fusion), channel_id=1, replica_groups=mesh['row'=32,'col'=8] {'row','col'}, use_global_device_ids=true, to_apply=%region_0.1 | all-reduce | flops 786432 | bytes 4718592 | tf_op jit(solution)/shard_map/psum | solution.py:57
  246.4 0.6 fusion.18
  247.0 0.8 copy.19
  247.7 0.0 reduce-scatter.2.cloned.1.call-done
  (25 shorter events, 0.2 us)
Async XLA Ops:
  7.2 101.8 %copy-start = (bf16[128,3072]{1,0:T(8,128)(2,1)S(1)}, bf16[128,3072]{1,0:T(8,128)(2,1)}, u32[]{:S(2)}) copy-start(bf16[128,3072]{1,0:T(8,128)(2,1)} %param.12) | copy-start | bytes 2359300
  7.2 14.2 %copy-start.1 = (bf16[800,120]{1,0:T(8,128)(2,1)S(1)}, bf16[800,120]{1,0:T(8,128)(2,1)}, u32[]{:S(2)}) copy-start(bf16[800,120]{1,0:T(8,128)(2,1)} %param.15) | copy-start | bytes 576004
  8.9 43.8 %all-to-all-start = ((bf16[128,32,8]{0,2,1:T(8,128)(2,1)}), bf16[128,32,8]{0,2,1:T(8,128)(2,1)S(1)}, u32[]{:S(2)}, u32[]{:S(2)}) async-start(bf16[128,32,8]{0,2,1:T(8,128)(2,1)} %bitcast.4), calls=%async_computation | async-start | bytes 131072 | tf_op jit(solution)/shard_map/all_to_all | solution.py:64
  19.3 228.5 %reduce-scatter.2.cloned.1.call-start = ((), (), s32[]{:S(2)}) async-start(), calls=%async_computation.2 | async-start | bytes 3686400 | tf_op jit(solution)/shard_map/reduce_scatter | solution.py:68
  108.3 0.7 copy-start.3
  110.6 2.4 copy-start.2
Sparse Core Ops, SparseCore 0:
  108.4 78.8 reduce-scatter.1
where the time goes:
time: 255 us
  blocking collectives  133 us (52%)
  matrix products  51.2 us (20%)
  local copies, waits for them, and re-layouts  32.1 us (13%)
  between operations  14.2 us (6%)
  other arithmetic  13.1 us (5%)
  starting transfers between devices  10.5 us (4%)
    psum x1, blocking collectives, per_device(): pivot_rows = lax.psum(contribution, ('row', 'col')).astype(jnp.bfloat16)  133 us
    dot_general x8, matrix products, one_block(): jnp.einsum('pi,vpm->vim', coeff_block, spread, preferred_element_type=jnp...  50.6 us
    gather x1, local copies, waits for them, and re-layouts, half_transform(): jnp.take(occupied, second_ao, axis=0)  12.1 us
    gather x1, local copies, waits for them, and re-layouts, half_transform(): occ_first = jnp.take(occupied, first_ao, axis=0)  12.1 us
    all_to_all x1, starting transfers between devices, per_device(): lax.all_to_all(grouped, 'row', split_axis=1, concat_axis=0, tiled=True)  10.4 us
    unnamed x12, local copies, waits for them, and re-layouts  6.15 us
  transfers between devices with their start and end apart: 2, of which 0 were waited for; matrix products, arithmetic and copies ran while one was open for 15% of the time, Pallas kernels for 0%

commit v1 on v0

--- a/solution.py
+++ b/solution.py
@@ -54,7 +54,7 @@
     owned = owner == own_index
     picked = jnp.take(prior, local_rows, axis=0).astype(jnp.float32)
     contribution = jnp.where(owned[:, None], picked, jnp.zeros_like(picked))
-    pivot_rows = lax.psum(contribution, ("row", "col")).astype(jnp.bfloat16)
+    pivot_rows = lax.psum(lax.psum(contribution, "col"), "row").astype(jnp.bfloat16)
     updated = panel - lax.dot_general(
         prior, pivot_rows, (((1,), (1,)), ((), ())), preferred_element_type=jnp.float32
     )

time: 255 us -> 368 us (1.44); the launches traced: 255 us -> 364 us
  waiting for transfers between devices: 0.02 us -> 59.3 us
  blocking collectives: 133 us -> 182 us
    psum x0 -> x1, waiting for transfers between devices: none -> 59.3 us  [per_device(): lax.psum(contribution, 'col')]
    psum x1, blocking collectives: 133 us -> 182 us  [per_device(): lax.psum(lax.psum(contribution, 'col'), 'row').astype(jnp.bfloat16)]
  transfers between devices with their start and end apart: 2 -> 3, of which waited for: 0 -> 1; matrix products, arithmetic and copies ran while one was open for 15% -> 26% of each run, Pallas kernels for 0% -> 0%
where the time goes in v1:
time: 368 us; the launch traced here: 364 us
  blocking collectives  182 us (49%)
  waiting for transfers between devices  59.3 us (16%)
  matrix products  51.4 us (14%)
  local copies, waits for them, and re-layouts  32.2 us (9%)
  between operations  14.2 us (4%)
  other arithmetic  13.9 us (4%)
  starting transfers between devices  10.5 us (3%)
    psum x1, blocking collectives, per_device(): lax.psum(lax.psum(contribution, 'col'), 'row').astype(jnp.bfloat16)  182 us
    psum x1, waiting for transfers between devices, per_device(): lax.psum(contribution, 'col')  59.3 us
    dot_general x8, matrix products, one_block(): jnp.einsum('pi,vpm->vim', coeff_block, spread, preferred_element_type=jnp...  50.9 us
    gather x1, local copies, waits for them, and re-layouts, half_transform(): jnp.take(occupied, second_ao, axis=0)  12.1 us
    gather x1, local copies, waits for them, and re-layouts, half_transform(): occ_first = jnp.take(occupied, first_ao, axis=0)  12.1 us
    all_to_all x1, starting transfers between devices, per_device(): lax.all_to_all(grouped, 'row', split_axis=1, concat_axis=0, tiled=True)  10.4 us
  transfers between devices with their start and end apart: 3, of which 1 were waited for; matrix products, arithmetic and copies ran while one was open for 26% of the time, Pallas kernels for 0%

profile of v1, /device:TPU:32, one launch (start us, length us, event | category | flops | bytes accessed | tf_op | source)
XLA Modules:
  0.0 363.6 jit_solution(9890308107096889617)
XLA Ops:
  7.2 0.0 copy-start
  7.2 1.6 copy.17
  8.8 10.4 %all-to-all-start = ((bf16[128,32,8]{0,2,1:T(8,128)(2,1)}), bf16[128,32,8]{0,2,1:T(8,128)(2,1)S(1)}, u32[]{:S(2)}, u32[]{:S(2)}) async-start(bf16[128,32,8]{0,2,1:T(8,128)(2,1)} %bitcast.4), calls=%async_computation | async-start | bytes 131072 | tf_op jit(solution)/shard_map/all_to_all | solution.py:64
  19.2 0.0 all-reduce.3.cloned.1.call-start
  19.3 0.7 compare_and_fusion.2
  20.0 0.0 copy-done
  20.0 1.6 gather_fusion
  21.6 0.0 copy-start.1
  21.6 2.4 convert_select_fusion
  24.0 0.0 all-reduce.3.cloned.1.call-update
  24.1 0.0 reduce-scatter.2.cloned.1.call-start
  24.1 1.0 broadcast_remainder_fusion
  25.1 1.0 compare_reduce_fusion
  26.2 0.0 copy-done.1
  26.2 12.1 %gather_fusion.2 = bf16[4096,120]{1,0:T(8,128)(2,1)S(1)} fusion(bf16[800,120]{1,0:T(8,128)(2,1)S(1)} %copy-done.1, s32[4096]{0:T(1024)S(1)} %get-tuple-element.172), kind=kCustom, calls=%fused_computation.1.clone | custom fusion | bytes 1982464 | tf_op jit(solution)/shard_map/jit(_take)/gather | solution.py:16
  38.3 12.1 %gather_fusion.1 = bf16[4096,120]{1,0:T(8,128)(2,1)S(1)} fusion(bf16[800,120]{1,0:T(8,128)(2,1)S(1)} %copy-done.1, s32[4096]{0:T(1024)S(1)} %fusion.21), kind=kCustom, calls=%fused_computation.clone | custom fusion | bytes 1982464 | tf_op jit(solution)/shard_map/jit(_take)/gather | solution.py:14
  50.5 2.1 broadcast_select_fusion
  52.6 1.4 select_select_fusion
  54.0 0.4 pad_maximum_fusion
  54.4 2.9 copy.18
  57.3 0.0 all-to-all-done
  57.4 55.9 %while.14 = (s32[]{:T(128)}, f32[8,120,800]{1,2,0:T(8,128)}, s32[8192]{0:T(1024)S(1)}, bf16[8192,8]{0,1:T(8,128)(2,1)S(1)}, bf16[8192,120]{0,1:T(8,128)(2,1)}, /*index=5*/s32[]{:T(128)}, s32[]{:T(128)}, s32[]{:T(128)}, s32[]{:T(128)}) while((s32[]{:T(128)}, f32[8,120,800]{1,2,0:T(8,128)}, s32[8192]{0:T(1024)S(1)}, ...), condition=%wide.region_3.5_spmd.clone, body=%wide.region_2.4_spmd.clone.sunk | while | flops 1581772800 | bytes 8294561 | solution.py:44
  57.4 0.6 iota_compare_fusion.2
  58.0 5.9 %bitcast_add_fusion.2 = f32[8,120,800]{1,2,0:T(8,128)} fusion(f32[8,120,800]{1,2,0:T(8,128)} %get-tuple-element.216, pred[1024,800]{0,1:T(8,128)(4,1)S(1)} %iota_compare_fusion.2, bf16[8,1024]{1,0:T(8,128)(2,1)S(1)} %dynamic-slice_bitcast_fusion.2, pred[]{:T(512)S(6)} %compare.6, bf16[8192,120]{0,1:T(8,128)(2,1)} %get-tuple-element.228, ...), kind=kOutput, calls=%fused_computation.9.clone.1 | convolution fusion | flops 1580953600 | bytes 7430149 | tf_op jit(solution)/shard_map/while/body/eval_jaxpr/pi,vpm->vim/dot_general | solution.py:39
  64.0 0.6 iota_compare_fusion.2
  64.6 6.4 %bitcast_add_fusion.2 = f32[8,120,800]{1,2,0:T(8,128)} fusion(f32[8,120,800]{1,2,0:T(8,128)} %get-tuple-element.216, pred[1024,800]{0,1:T(8,128)(4,1)S(1)} %iota_compare_fusion.2, bf16[8,1024]{1,0:T(8,128)(2,1)S(1)} %dynamic-slice_bitcast_fusion.2, pred[]{:T(512)S(6)} %compare.6, bf16[8192,120]{0,1:T(8,128)(2,1)} %get-tuple-element.228, ...), kind=kOutput, calls=%fused_computation.9.clone.1 | convolution fusion | flops 1580953600 | bytes 7430149 | tf_op jit(solution)/shard_map/while/body/eval_jaxpr/pi,vpm->vim/dot_general | solution.py:39
  71.0 0.6 iota_compare_fusion.2
  71.6 6.4 %bitcast_add_fusion.2 = f32[8,120,800]{1,2,0:T(8,128)} fusion(f32[8,120,800]{1,2,0:T(8,128)} %get-tuple-element.216, pred[1024,800]{0,1:T(8,128)(4,1)S(1)} %iota_compare_fusion.2, bf16[8,1024]{1,0:T(8,128)(2,1)S(1)} %dynamic-slice_bitcast_fusion.2, pred[]{:T(512)S(6)} %compare.6, bf16[8192,120]{0,1:T(8,128)(2,1)} %get-tuple-element.228, ...), kind=kOutput, calls=%fused_computation.9.clone.1 | convolution fusion | flops 1580953600 | bytes 7430149 | tf_op jit(solution)/shard_map/while/body/eval_jaxpr/pi,vpm->vim/dot_general | solution.py:39
  78.1 0.6 iota_compare_fusion.2
  78.7 6.4 %bitcast_add_fusion.2 = f32[8,120,800]{1,2,0:T(8,128)} fusion(f32[8,120,800]{1,2,0:T(8,128)} %get-tuple-element.216, pred[1024,800]{0,1:T(8,128)(4,1)S(1)} %iota_compare_fusion.2, bf16[8,1024]{1,0:T(8,128)(2,1)S(1)} %dynamic-slice_bitcast_fusion.2, pred[]{:T(512)S(6)} %compare.6, bf16[8192,120]{0,1:T(8,128)(2,1)} %get-tuple-element.228, ...), kind=kOutput, calls=%fused_computation.9.clone.1 | convolution fusion | flops 1580953600 | bytes 7430149 | tf_op jit(solution)/shard_map/while/body/eval_jaxpr/pi,vpm->vim/dot_general | solution.py:39
  85.1 0.6 iota_compare_fusion.2
  85.7 6.4 %bitcast_add_fusion.2 = f32[8,120,800]{1,2,0:T(8,128)} fusion(f32[8,120,800]{1,2,0:T(8,128)} %get-tuple-element.216, pred[1024,800]{0,1:T(8,128)(4,1)S(1)} %iota_compare_fusion.2, bf16[8,1024]{1,0:T(8,128)(2,1)S(1)} %dynamic-slice_bitcast_fusion.2, pred[]{:T(512)S(6)} %compare.6, bf16[8192,120]{0,1:T(8,128)(2,1)} %get-tuple-element.228, ...), kind=kOutput, calls=%fused_computation.9.clone.1 | convolution fusion | flops 1580953600 | bytes 7430149 | tf_op jit(solution)/shard_map/while/body/eval_jaxpr/pi,vpm->vim/dot_general | solution.py:39
  92.1 0.6 iota_compare_fusion.2
  92.8 6.4 %bitcast_add_fusion.2 = f32[8,120,800]{1,2,0:T(8,128)} fusion(f32[8,120,800]{1,2,0:T(8,128)} %get-tuple-element.216, pred[1024,800]{0,1:T(8,128)(4,1)S(1)} %iota_compare_fusion.2, bf16[8,1024]{1,0:T(8,128)(2,1)S(1)} %dynamic-slice_bitcast_fusion.2, pred[]{:T(512)S(6)} %compare.6, bf16[8192,120]{0,1:T(8,128)(2,1)} %get-tuple-element.228, ...), kind=kOutput, calls=%fused_computation.9.clone.1 | convolution fusion | flops 1580953600 | bytes 7430149 | tf_op jit(solution)/shard_map/while/body/eval_jaxpr/pi,vpm->vim/dot_general | solution.py:39
  99.2 0.6 iota_compare_fusion.2
  99.8 6.4 %bitcast_add_fusion.2 = f32[8,120,800]{1,2,0:T(8,128)} fusion(f32[8,120,800]{1,2,0:T(8,128)} %get-tuple-element.216, pred[1024,800]{0,1:T(8,128)(4,1)S(1)} %iota_compare_fusion.2, bf16[8,1024]{1,0:T(8,128)(2,1)S(1)} %dynamic-slice_bitcast_fusion.2, pred[]{:T(512)S(6)} %compare.6, bf16[8192,120]{0,1:T(8,128)(2,1)} %get-tuple-element.228, ...), kind=kOutput, calls=%fused_computation.9.clone.1 | convolution fusion | flops 1580953600 | bytes 7430149 | tf_op jit(solution)/shard_map/while/body/eval_jaxpr/pi,vpm->vim/dot_general | solution.py:39
  106.2 0.6 iota_compare_fusion.2
  106.9 6.4 %bitcast_add_fusion.2 = f32[8,120,800]{1,2,0:T(8,128)} fusion(f32[8,120,800]{1,2,0:T(8,128)} %get-tuple-element.216, pred[1024,800]{0,1:T(8,128)(4,1)S(1)} %iota_compare_fusion.2, bf16[8,1024]{1,0:T(8,128)(2,1)S(1)} %dynamic-slice_bitcast_fusion.2, pred[]{:T(512)S(6)} %compare.6, bf16[8192,120]{0,1:T(8,128)(2,1)} %get-tuple-element.228, ...), kind=kOutput, calls=%fused_computation.9.clone.1 | convolution fusion | flops 1580953600 | bytes 7430149 | tf_op jit(solution)/shard_map/while/body/eval_jaxpr/pi,vpm->vim/dot_general | solution.py:39
  113.3 0.0 copy-start.2
  113.3 0.0 reduce-scatter.2.cloned.1.call-update
  113.3 0.9 copy-done.2
  114.2 0.1 copy.16
  114.3 59.3 %all-reduce.3.cloned.1.call-done = f32[256,3072]{1,0:T(8,128)} async-done(((f32[256,3072]{1,0:T(8,128)}), f32[256,3072]{1,0:T(8,128)}) %all-reduce.3.cloned.1.call-update) | async-done | bytes 3145744 | tf_op jit(solution)/shard_map/psum | solution.py:57
  173.5 181.9 %all-reduce.4 = bf16[256,3072]{1,0:T(8,128)(2,1)S(1)} all-reduce(f32[256,3072]{1,0:T(8,128)} %all-reduce.3.cloned.1.call-done), channel_id=1, replica_groups=mesh['row'=32,'col'=8] {'row'}, use_global_device_ids=true, to_apply=%region_1.2 | all-reduce | flops 786432 | bytes 4718592 | tf_op jit(solution)/shard_map/psum | solution.py:57
  355.5 0.6 fusion.18
  356.0 0.8 copy.19
  356.8 0.0 reduce-scatter.2.cloned.1.call-done
  (24 shorter events, 0.2 us)
Async XLA Ops:
  7.2 12.9 %copy-start = (bf16[128,3072]{1,0:T(8,128)(2,1)S(1)}, bf16[128,3072]{1,0:T(8,128)(2,1)}, u32[]{:S(2)}) copy-start(bf16[128,3072]{1,0:T(8,128)(2,1)} %param.12) | copy-start | bytes 2359300
  8.8 48.5 %all-to-all-start = ((bf16[128,32,8]{0,2,1:T(8,128)(2,1)}), bf16[128,32,8]{0,2,1:T(8,128)(2,1)S(1)}, u32[]{:S(2)}, u32[]{:S(2)}) async-start(bf16[128,32,8]{0,2,1:T(8,128)(2,1)} %bitcast.4), calls=%async_computation | async-start | bytes 131072 | tf_op jit(solution)/shard_map/all_to_all | solution.py:64
  19.2 154.3 %all-reduce.3.cloned.1.call-start = ((), (), s32[]{:S(2)}) async-start(), calls=%async_computation.2 | async-start | bytes 6291456 | tf_op jit(solution)/shard_map/psum | solution.py:57
  21.6 4.6 %copy-start.1 = (bf16[800,120]{1,0:T(8,128)(2,1)S(1)}, bf16[800,120]{1,0:T(8,128)(2,1)}, u32[]{:S(2)}) copy-start(bf16[800,120]{1,0:T(8,128)(2,1)} %param.15) | copy-start | bytes 576004
  24.1 332.7 %reduce-scatter.2.cloned.1.call-start = ((), (), s32[]{:S(2)}) async-start(), calls=%async_computation.3 | async-start | bytes 3686400 | tf_op jit(solution)/shard_map/reduce_scatter | solution.py:68
  113.3 0.9 copy-start.2
Sparse Core Ops, SparseCore 0:
  24.2 149.3 all-reduce.2
  176.7 106.9 reduce-scatter.1
